TPU v7x, 32 devices: a whole 2x2x4 slice. The times are simulated.
32 devices in a mesh: row: 4 (over z), col: 4 (over y, core), rep: 2 (over x).
Axes of the slice: x: 2, y: 2, z: 4, core: 2. Of those that a mesh axis runs over, the one named last changes fastest.
Arguments:
- amplitudes: bfloat16 [1024, 8192], P('row', 'col'), may hold values from -6 to 6
- intermediate: bfloat16 [8192, 1024], P('row', 'col'), may hold values from -0.0625 to 0.0625
Outputs:
- residual: float32 [8, 4, 32, 1024], P(None, 'col', None, ('row', 'rep'))
All inputs are finite; a program needn't handle non-finite values.
Results may differ from a plain program's by a relative error of at most 0.0029.
Values may be sent and summed in bfloat16 or wider, within the bound.
A program may use at most 128 MiB of HBM per device.

v0:
```python
import jax
import jax.numpy as jnp
from jax import lax
from jax.sharding import PartitionSpec as P


def local(amplitudes, intermediate):
    rows_axis = lax.axis_size("row")
    cols_axis = lax.axis_size("col")
    depth_axis = lax.axis_size("rep")
    layer_index = lax.axis_index("rep")
    owner_rows = rows_axis * depth_axis
    fold_count = owner_rows // cols_axis
    local_rows = amplitudes.shape[0]
    band_rows = local_rows // depth_axis
    local_cols = intermediate.shape[1]
    slice_width = local_cols // owner_rows
    own_rows = lax.dynamic_slice_in_dim(amplitudes, layer_index * band_rows, band_rows, 0)
    all_weights = lax.all_gather(intermediate, "row", axis=0, tiled=True)
    summed = jnp.dot(
        lax.all_gather(own_rows, "col", axis=1, tiled=True),
        all_weights,
        preferred_element_type=jnp.float32,
    )
    cycle = summed.astype(jnp.bfloat16)
    spread_block = cycle.reshape(band_rows, fold_count, cols_axis, slice_width)
    direct = lax.all_to_all(spread_block, "col", split_axis=2, concat_axis=1, tiled=True).reshape(
        band_rows, owner_rows, slice_width
    )
    stacked = cycle.reshape(cols_axis, slice_width, fold_count, cols_axis * slice_width)
    mirror = lax.all_to_all(
        lax.all_to_all(stacked, "col", split_axis=0, concat_axis=2, tiled=True),
        ("row", "rep"),
        split_axis=2,
        concat_axis=0,
        tiled=True,
    )
    mirror_part = mirror.reshape(owner_rows, slice_width, band_rows).astype(jnp.float32)
    direct_part = jnp.transpose(direct, (1, 2, 0)).astype(jnp.float32)
    return (mirror_part + direct_part).reshape(owner_rows, 1, slice_width, band_rows)


def solution(mesh):
    in_specs = (P("row", "col"), P("row", "col"))
    out_specs = P(None, "col", None, ("row", "rep"))
    return jax.shard_map(local, mesh=mesh, in_specs=in_specs, out_specs=out_specs, check_vma=False)
```

profile of v0, /device:TPU:0, one launch (start us, length us, event | category | flops | bytes accessed | tf_op | source)
XLA Modules:
  0.0 153.2 jit_solution(1492077100807773133)
XLA Ops:
  6.5 0.0 copy-start
  6.5 0.0 all-gather.3.cloned.1.call-start
  6.5 1.2 copy-done
  7.8 0.9 constant_dynamic-slice_fusion
  8.6 0.0 all-gather.3.cloned.1.call-update
  8.6 0.0 all-gather.5.cloned.1.call-start
  8.7 0.7 all-gather.5.cloned.1.call-update
  9.4 24.8 %all-gather.3.cloned.1.call-done = bf16[128,8192]{1,0:T(8,128)(2,1)} async-done(((bf16[128,2048]{1,0:T(8,128)(2,1)}), bf16[128,8192]{1,0:T(8,128)(2,1)}) %all-gather.3.cloned.1.call-update) | async-done | bytes 2097168 | tf_op jit(solution)/shard_map/all_gather | solution.py:21
  34.2 82.3 %all-gather.5.cloned.1.call-done = bf16[8192,256]{1,0:T(8,128)(2,1)} async-done(((bf16[2048,256]{1,0:T(8,128)(2,1)}), bf16[8192,256]{1,0:T(8,128)(2,1)}) %all-gather.5.cloned.1.call-update) | async-done | bytes 4194320 | tf_op jit(solution)/shard_map/all_gather | solution.py:19
  116.6 3.5 %convolution_convert_fusion = bf16[128,256]{1,0:T(8,128)(2,1)S(1)} fusion(bf16[128,8192]{1,0:T(8,128)(2,1)} %all-gather.3.cloned.1.call-done, bf16[8192,256]{1,0:T(8,128)(2,1)} %all-gather.5.cloned.1.call-done), kind=kOutput, calls=%fused_computation | convolution fusion | flops 536903680 | bytes 6356992 | tf_op jit(solution)/shard_map/dot_general | solution.py:20
  120.1 0.7 reshape.21
  120.7 3.3 %all-to-all-start = ((bf16[4,32,2,128]{3,2,1,0:T(2,128)(2,1)}), bf16[4,32,2,128]{3,2,1,0:T(2,128)(2,1)S(1)}, u32[]{:S(2)}, u32[]{:S(2)}) async-start(bf16[4,32,2,128]{3,2,1,0:T(2,128)(2,1)} %reshape.21), calls=%async_computation | async-start | bytes 131072 | tf_op jit(solution)/shard_map/all_to_all | solution.py:32
  124.0 0.1 copy.13
  124.2 0.6 copy.14
  124.8 3.3 %all-to-all-done = bf16[4,32,2,128]{3,2,1,0:T(2,128)(2,1)S(1)} async-done(((bf16[4,32,2,128]{3,2,1,0:T(2,128)(2,1)}), bf16[4,32,2,128]{3,2,1,0:T(2,128)(2,1)S(1)}, u32[]{:S(2)}, u32[]{:S(2)}) %all-to-all-start) | async-done | bytes 65568 | tf_op jit(solution)/shard_map/all_to_all | solution.py:32
  128.1 3.3 %all-to-all-start.2 = ((bf16[128,2,4,32]{0,3,1,2:T(8,128)(2,1)}), bf16[128,2,4,32]{0,3,1,2:T(8,128)(2,1)S(1)}, u32[]{:S(2)}, u32[]{:S(2)}) async-start(bf16[128,2,4,32]{0,3,1,2:T(8,128)(2,1)} %copy.14), calls=%async_computation.2 | async-start | bytes 131072 | tf_op jit(solution)/shard_map/all_to_all | solution.py:27
  131.4 0.6 copy.11
  132.1 3.4 %all-to-all-done.2 = bf16[128,2,4,32]{0,3,1,2:T(8,128)(2,1)S(1)} async-done(((bf16[128,2,4,32]{0,3,1,2:T(8,128)(2,1)}), bf16[128,2,4,32]{0,3,1,2:T(8,128)(2,1)S(1)}, u32[]{:S(2)}, u32[]{:S(2)}) %all-to-all-start.2) | async-done | bytes 65568 | tf_op jit(solution)/shard_map/all_to_all | solution.py:27
  135.5 3.3 %all-to-all-start.1 = ((bf16[1,32,8,128]{3,1,0,2:T(8,128)(2,1)}), bf16[1,32,8,128]{3,1,0,2:T(8,128)(2,1)S(1)}, u32[]{:S(2)}, u32[]{:S(2)}) async-start(bf16[1,32,8,128]{3,1,0,2:T(8,128)(2,1)} %bitcast.2), calls=%async_computation.1 | async-start | bytes 131072 | tf_op jit(solution)/shard_map/all_to_all | solution.py:31
  138.9 6.8 %all-to-all-done.1 = bf16[1,32,8,128]{3,1,0,2:T(8,128)(2,1)S(1)} async-done(((bf16[1,32,8,128]{3,1,0,2:T(8,128)(2,1)}), bf16[1,32,8,128]{3,1,0,2:T(8,128)(2,1)S(1)}, u32[]{:S(2)}, u32[]{:S(2)}) %all-to-all-start.1) | async-done | bytes 65568 | tf_op jit(solution)/shard_map/all_to_all | solution.py:31
  145.7 0.7 bitcast_add_fusion
  (1 shorter events, 0.0 us)
Async XLA Ops:
  6.5 1.2 copy-start
  6.5 27.7 %all-gather.3.cloned.1.call-start = ((), (), s32[]{:S(2)}) async-start(), calls=%async_computation.3 | async-start | bytes 2621440 | tf_op jit(solution)/shard_map/all_gather | solution.py:21
  8.6 107.9 %all-gather.5.cloned.1.call-start = ((), (), s32[]{:S(2)}) async-start(), calls=%async_computation.4 | async-start | bytes 5242880 | tf_op jit(solution)/shard_map/all_gather | solution.py:19
  120.7 7.4 %all-to-all-start = ((bf16[4,32,2,128]{3,2,1,0:T(2,128)(2,1)}), bf16[4,32,2,128]{3,2,1,0:T(2,128)(2,1)S(1)}, u32[]{:S(2)}, u32[]{:S(2)}) async-start(bf16[4,32,2,128]{3,2,1,0:T(2,128)(2,1)} %reshape.21), calls=%async_computation | async-start | bytes 131072 | tf_op jit(solution)/shard_map/all_to_all | solution.py:32
  128.1 7.4 %all-to-all-start.2 = ((bf16[128,2,4,32]{0,3,1,2:T(8,128)(2,1)}), bf16[128,2,4,32]{0,3,1,2:T(8,128)(2,1)S(1)}, u32[]{:S(2)}, u32[]{:S(2)}) async-start(bf16[128,2,4,32]{0,3,1,2:T(8,128)(2,1)} %copy.14), calls=%async_computation.2 | async-start | bytes 131072 | tf_op jit(solution)/shard_map/all_to_all | solution.py:27
  135.5 10.2 %all-to-all-start.1 = ((bf16[1,32,8,128]{3,1,0,2:T(8,128)(2,1)}), bf16[1,32,8,128]{3,1,0,2:T(8,128)(2,1)S(1)}, u32[]{:S(2)}, u32[]{:S(2)}) async-start(bf16[1,32,8,128]{3,1,0,2:T(8,128)(2,1)} %bitcast.2), calls=%async_computation.1 | async-start | bytes 131072 | tf_op jit(solution)/shard_map/all_to_all | solution.py:31
Sparse Core Ops, SparseCore 0:
  8.9 25.2 all-gather.2
  35.8 80.7 all-gather.4
where the time goes:
time: 154 us; the launch traced here: 153 us
  waiting for transfers between devices  121 us (79%)
  between operations  13.4 us (9%)
  starting transfers between devices  9.96 us (6%)
  local copies, waits for them, and re-layouts  4.12 us (3%)
  matrix products  3.53 us (2%)
    all_gather x1, waiting for transfers between devices, local(): all_weights = lax.all_gather(intermediate, 'row', axis=0, tiled=True)  82.3 us
    all_gather x1, waiting for transfers between devices, local(): lax.all_gather(own_rows, 'col', axis=1, tiled=True)  24.8 us
    all_to_all x1, waiting for transfers between devices, local(): lax.all_to_all(lax.all_to_all(stacked, 'col', split_axis=0, concat_axis=2...  6.82 us
    dot_general x1, matrix products, local(): jnp.dot(lax.all_gather(own_rows, 'col', axis=1, tiled=True), all_weights,...  3.53 us
    all_to_all x1, waiting for transfers between devices, local(): lax.all_to_all(spread_block, 'col', split_axis=2, concat_axis=1, tiled=True)  3.44 us
    all_to_all x1, starting transfers between devices, local(): lax.all_to_all(lax.all_to_all(stacked, 'col', split_axis=0, concat_axis=2...  3.35 us
    all_to_all x1, waiting for transfers between devices, local(): lax.all_to_all(stacked, 'col', split_axis=0, concat_axis=2, tiled=True)  3.33 us
    all_to_all x1, starting transfers between devices, local(): lax.all_to_all(spread_block, 'col', split_axis=2, concat_axis=1, tiled=True)  3.29 us
  transfers between devices with their start and end apart: 5, of which 5 were waited for; matrix products, arithmetic and copies ran while one was open for 1% of the time, Pallas kernels for 0%

commit v1 on v0

--- a/solution.py
+++ b/solution.py
@@ -1,10 +1,16 @@
+import functools
+
 import jax
 import jax.numpy as jnp
 from jax import lax
+from jax.experimental import pallas as pl
+from jax.experimental.pallas import tpu as pltpu
 from jax.sharding import PartitionSpec as P
 
-
-def local(amplitudes, intermediate):
+MESH = pl.DeviceIdType.MESH
+
+
+def general(amplitudes, intermediate):
     rows_axis = lax.axis_size("row")
     cols_axis = lax.axis_size("col")
     depth_axis = lax.axis_size("rep")
@@ -40,7 +46,260 @@
     return (mirror_part + direct_part).reshape(owner_rows, 1, slice_width, band_rows)
 
 
+def kernel(
+    sizes, a_hbm, w_hbm, o_ref,
+    a_v, w_v, relay, abuf, wbuf, p0, p1, r0, r1, cyc, spread, perm, drecv, mrecv,
+    in_sem, s_rly, s_a, s_b, s_w1, s_w2, s_fw, s_r0, s_r1, s_m, s_d,
+    q_rly, q_a, q_w1, q_w2, q_r0, q_r1, q_m, q_d,
+):
+    rows, cols, depth, chunks = sizes
+    r, c, x = lax.axis_index("row"), lax.axis_index("col"), lax.axis_index("rep")
+    y, u = c // 2, c % 2
+    oy, ou, ox = 1 - y, 1 - u, 1 - x
+    band, kc = a_v.shape
+    width = w_v.shape[1]
+    sub = band // (2 * depth)
+    half = kc // 2
+    slab = kc // (2 * chunks)
+    strip = o_ref.shape[2]
+    lanes = o_ref.shape[3]
+    groups = width // (cols * strip)
+    f32 = jnp.float32
+
+    loads = (
+        pltpu.make_async_copy(a_hbm, a_v, in_sem.at[0]),
+        pltpu.make_async_copy(w_hbm, w_v, in_sem.at[1]),
+    )
+    for load in loads:
+        load.start()
+
+    barrier = pltpu.get_barrier_semaphore()
+    total = rows * cols * depth
+    me = (r * cols + c) * depth + x
+
+    def greet(step, carry):
+        other = (me + step) % total
+        pl.semaphore_signal(
+            barrier,
+            inc=1,
+            device_id=(other // (cols * depth), (other // depth) % cols, other % depth),
+            device_id_type=MESH,
+        )
+        return carry
+
+    lax.fori_loop(1, total, greet, 0)
+
+    src = lax.broadcasted_iota(jnp.int32, (2 * width, 2 * width), 0)
+    dst = lax.broadcasted_iota(jnp.int32, (2 * width, 2 * width), 1)
+    lane_in = dst % strip
+    grp = (dst // strip) % groups
+    blk = (dst // (strip * groups)) % 2
+    own = dst // (2 * strip * groups)
+    perm[...] = jnp.where(
+        src == blk * width + grp * (cols * strip) + own * strip + lane_in, 1.0, 0.0
+    ).astype(jnp.bfloat16)
+
+    pl.semaphore_wait(barrier, total - 1)
+    loads[0].wait()
+
+    def remote(source, target, send, recv, to):
+        return pltpu.make_async_remote_copy(
+            src_ref=source, dst_ref=target, send_sem=send, recv_sem=recv,
+            device_id=to, device_id_type=MESH,
+        )
+
+    def arrived(target, recv):
+        pltpu.make_async_copy(target, target, recv).wait()
+
+    pending = []
+
+    def send(source, target, ssem, rsem, to, same=None):
+        copy = remote(source, target, ssem, rsem, to)
+        if same is None:
+            copy.start()
+            pending.append((copy, None))
+            return
+
+        @pl.when(same)
+        def _():
+            pltpu.make_async_copy(source, target, rsem).start()
+
+        @pl.when(jnp.logical_not(same))
+        def _():
+            copy.start()
+
+        pending.append((copy, jnp.logical_not(same)))
+
+    def rowset(side):
+        return pl.ds(pl.multiple_of((x * 2 + side) * sub, sub), sub)
+
+    def khalf(v):
+        return pl.ds(v * half, half)
+
+    for v in range(2):
+        send(a_v.at[rowset(oy), khalf(v)], relay.at[:, khalf(v)], s_rly.at[v], q_rly.at[v], (r, oy * 2 + u, x))
+    for v in range(2):
+        send(
+            a_v.at[rowset(y), khalf(v)], abuf.at[r, :, khalf(v)], s_a.at[v], q_a.at[r, v],
+            (c, y * 2 + v, x), jnp.logical_and(c == r, u == v),
+        )
+    loads[1].wait()
+
+    def wrows(side, n):
+        return pl.ds(pl.multiple_of(side * half + n * slab, slab), slab)
+
+    for n in range(chunks):
+        send(w_v.at[wrows(x, n)], wbuf.at[wrows(x, n)], s_w1.at[n], q_w1.at[n], (r, oy * 2 + u, x))
+
+    far = oy * 2 + u
+    for v in range(2):
+        arrived(relay.at[:, khalf(v)], q_rly.at[v])
+        send(
+            relay.at[:, khalf(v)], abuf.at[r, :, khalf(v)], s_b.at[v], q_a.at[r, v],
+            (far, y * 2 + v, x), jnp.logical_and(far == r, u == v),
+        )
+
+    order = (r, r + 1 - 2 * (r % 2), (r + rows // 2) % rows, rows - 1 - r)
+
+    def forward_w(n):
+        arrived(wbuf.at[wrows(x, n)], q_w1.at[n])
+        send(wbuf.at[wrows(x, n)], wbuf.at[wrows(x, n)], s_w2.at[n], q_w2.at[n], (r, c, ox))
+
+    def forward_a(i):
+        mine = pl.ds(pl.multiple_of(u * half, half), half)
+        arrived(abuf.at[i, :, mine], q_a.at[i, u])
+        send(abuf.at[i, :, mine], abuf.at[i, :, mine], s_fw.at[i], q_a.at[i, u], (r, y * 2 + ou, x))
+
+    def product(i, d):
+        theirs = pl.ds(pl.multiple_of(ou * half, half), half)
+        arrived(abuf.at[i, :, theirs], q_a.at[i, ou])
+        p0[i] = jnp.dot(abuf[i], w_v[...], preferred_element_type=f32)
+        if d > 0:
+            send(p0.at[i], r0.at[r], s_r0.at[i], q_r0.at[r], (i, c, x))
+
+    steps = max(rows, chunks)
+    for d in range(steps):
+        if d < rows:
+            forward_a(order[d])
+        if d < chunks:
+            forward_w(d)
+        if 0 < d <= rows:
+            product(order[d - 1], d - 1)
+    if rows == steps:
+        product(order[rows - 1], rows - 1)
+
+    def add_product(side, n, first):
+        at = pl.ds(pl.multiple_of(side * half + n * slab, slab), slab)
+        part = jnp.dot(
+            abuf[:, :, at].reshape(rows * sub, slab), wbuf[at, :], preferred_element_type=f32
+        ).reshape(rows, sub, width)
+        p1[...] = part if first else p1[...] + part
+
+    for n in range(chunks):
+        add_product(x, n, n == 0)
+    for n in range(chunks):
+        arrived(wbuf.at[wrows(ox, n)], q_w2.at[n])
+        add_product(ox, n, False)
+    for d in range(1, rows):
+        i = order[d]
+        send(p1.at[i], r1.at[r], s_r1.at[i], q_r1.at[r], (i, c, x))
+
+    def finish(part, got, sems, q, block):
+        value = part[r]
+        for d in range(1, rows):
+            i = order[d]
+            arrived(got.at[i], sems.at[i])
+            value = value + got[i]
+        cyc[block] = value.astype(jnp.bfloat16)
+        owner = block * 2 + u
+        for px in range(depth):
+            for pu in range(2):
+                same = jnp.logical_and(jnp.logical_and(owner == r, px == x), pu == u)
+                send(
+                    cyc.at[block, pl.ds(pu * strip, strip), pl.ds(px * lanes, lanes)],
+                    mrecv.at[r * depth + x],
+                    s_m.at[q, px, pu], q_m.at[r * depth + x], (owner, y * 2 + pu, px), same,
+                )
+
+    finish(p0, r0, q_r0, 0, y)
+    finish(p1, r1, q_r1, 1, oy)
+
+    turned = jnp.dot(cyc[0], perm[pl.ds(0, width), :], preferred_element_type=f32)
+    turned = turned + jnp.dot(cyc[1], perm[pl.ds(width, width), :], preferred_element_type=f32)
+    for to in range(cols):
+        spread[to] = turned[:, to * lanes:(to + 1) * lanes].astype(jnp.bfloat16)
+    place = pl.ds(pl.multiple_of(y * sub, sub), sub)
+    for to in range(cols):
+        send(spread.at[to], drecv.at[u, place, :], s_d.at[to], q_d.at[u, y], (r, to, x), c == to)
+
+    for i in range(rows * depth):
+        arrived(mrecv.at[i], q_m.at[i])
+    for pu in range(2):
+        for py in range(2):
+            arrived(drecv.at[pu, pl.ds(py * sub, sub), :], q_d.at[pu, py])
+        flipped = jnp.transpose(drecv[pu].astype(f32))
+        for py in range(2):
+            for g in range(groups):
+                at = (py * groups + g) * strip
+                a = (py * 2 + pu) * groups + g
+                o_ref[a, 0] = mrecv[a].astype(f32) + flipped[at:at + strip, :]
+
+    for copy, sent in pending:
+        if sent is None:
+            copy.wait_send()
+        else:
+            pl.when(sent)(copy.wait_send)
+
+
+def planned(sizes, amplitudes, intermediate):
+    rows, cols, depth, chunks = sizes
+    band, kc = amplitudes.shape
+    width = intermediate.shape[1]
+    sub = band // (2 * depth)
+    owners = rows * depth
+    strip = width // owners
+    lanes = band // depth
+    bf16, f32 = jnp.bfloat16, jnp.float32
+    dma = pltpu.SemaphoreType.DMA
+    return pl.pallas_call(
+        functools.partial(kernel, sizes),
+        out_shape=jax.ShapeDtypeStruct((owners, 1, strip, lanes), f32),
+        in_specs=[pl.BlockSpec(memory_space=pl.ANY)] * 2,
+        out_specs=pl.BlockSpec(memory_space=pltpu.VMEM),
+        scratch_shapes=[
+            pltpu.VMEM((band, kc), bf16),
+            pltpu.VMEM((kc, width), bf16),
+            pltpu.VMEM((sub, kc), bf16),
+            pltpu.VMEM((rows, sub, kc), bf16),
+            pltpu.VMEM((kc, width), bf16),
+            pltpu.VMEM((rows, sub, width), f32),
+            pltpu.VMEM((rows, sub, width), f32),
+            pltpu.VMEM((rows, sub, width), f32),
+            pltpu.VMEM((rows, sub, width), f32),
+            pltpu.VMEM((2, sub, width), bf16),
+            pltpu.VMEM((cols, sub, lanes), bf16),
+            pltpu.VMEM((2 * width, 2 * width), bf16),
+            pltpu.VMEM((2, 2 * sub, lanes), bf16),
+            pltpu.VMEM((owners, strip, lanes), bf16),
+            dma((2,)), dma((2,)), dma((2,)), dma((2,)), dma((chunks,)), dma((chunks,)),
+            dma((rows,)), dma((rows,)), dma((rows,)), dma((2, depth, 2)), dma((cols,)),
+            dma((2,)), dma((rows, 2)), dma((chunks,)), dma((chunks,)),
+            dma((rows,)), dma((rows,)), dma((owners,)), dma((2, 2)),
+        ],
+        compiler_params=pltpu.CompilerParams(collective_id=0, has_side_effects=True),
+    )(amplitudes, intermediate)
+
+
 def solution(mesh):
+    rows, cols, depth = (mesh.shape[name] for name in ("row", "col", "rep"))
+
+    def local(amplitudes, intermediate):
+        square = rows == cols == 2 * depth and depth == 2
+        fits = amplitudes.shape[0] == intermediate.shape[1]
+        if square and fits:
+            return planned((rows, cols, depth, 4), amplitudes, intermediate)
+        return general(amplitudes, intermediate)
+
     in_specs = (P("row", "col"), P("row", "col"))
     out_specs = P(None, "col", None, ("row", "rep"))
     return jax.shard_map(local, mesh=mesh, in_specs=in_specs, out_specs=out_specs, check_vma=False)

time: 154 us -> 45.1 us (0.29)
  the two profiles are of different devices: /device:TPU:0 before, /device:TPU:5 now
where the time goes in v1:
time: 45.1 us; the launch traced here: 44.9 us
  Pallas kernels  43.4 us (96%)
  local copies, waits for them, and re-layouts  1.57 us (3%)
    pallas_call x1, Pallas kernels, planned(): pl.pallas_call(functools.partial(kernel, sizes), out_shape=jax.ShapeDtype...  43.4 us
    unnamed x1, local copies, waits for them, and re-layouts  1.57 us

profile of v1, /device:TPU:5, one launch (start us, length us, event | category | flops | bytes accessed | tf_op | source)
XLA Modules:
  0.0 44.9 jit_solution(7224698382801115128)
XLA Ops:
  0.0 43.4 %shard_map.28 = f32[8,1,32,128]{3,2,1,0:T(8,128)} custom-call(bf16[256,2048]{1,0:T(8,128)(2,1)} %a_hbm.1, bf16[2048,256]{1,0:T(8,128)(2,1)} %w_hbm.1), custom_call_target="tpu_custom_call" | custom-call | tf_op jit(solution)/shard_map/pallas_call | solution.py:264
  43.4 1.6 %copy.4 = f32[8,1,32,128]{3,2,1,0:T(8,128)} copy(f32[8,1,32,128]{3,2,1,0:T(8,128)} %shard_map.28) | data formatting | bytes 262144

commit v2 on v1

v2 whole, which is shorter than its diff:
```python
import functools

import jax
import jax.numpy as jnp
from jax import lax
from jax.experimental import pallas as pl
from jax.experimental.pallas import tpu as pltpu
from jax.sharding import PartitionSpec as P

MESH = pl.DeviceIdType.MESH


def general(amplitudes, intermediate):
    rows_axis = lax.axis_size("row")
    cols_axis = lax.axis_size("col")
    depth_axis = lax.axis_size("rep")
    layer_index = lax.axis_index("rep")
    owner_rows = rows_axis * depth_axis
    fold_count = owner_rows // cols_axis
    local_rows = amplitudes.shape[0]
    band_rows = local_rows // depth_axis
    local_cols = intermediate.shape[1]
    slice_width = local_cols // owner_rows
    own_rows = lax.dynamic_slice_in_dim(amplitudes, layer_index * band_rows, band_rows, 0)
    all_weights = lax.all_gather(intermediate, "row", axis=0, tiled=True)
    summed = jnp.dot(
        lax.all_gather(own_rows, "col", axis=1, tiled=True),
        all_weights,
        preferred_element_type=jnp.float32,
    )
    cycle = summed.astype(jnp.bfloat16)
    spread_block = cycle.reshape(band_rows, fold_count, cols_axis, slice_width)
    direct = lax.all_to_all(spread_block, "col", split_axis=2, concat_axis=1, tiled=True).reshape(
        band_rows, owner_rows, slice_width
    )
    stacked = cycle.reshape(cols_axis, slice_width, fold_count, cols_axis * slice_width)
    mirror = lax.all_to_all(
        lax.all_to_all(stacked, "col", split_axis=0, concat_axis=2, tiled=True),
        ("row", "rep"),
        split_axis=2,
        concat_axis=0,
        tiled=True,
    )
    mirror_part = mirror.reshape(owner_rows, slice_width, band_rows).astype(jnp.float32)
    direct_part = jnp.transpose(direct, (1, 2, 0)).astype(jnp.float32)
    return (mirror_part + direct_part).reshape(owner_rows, 1, slice_width, band_rows)


def kernel(
    sizes, a_hbm, w_hbm, o_ref,
    a_v, w_v, relay, abuf, wbuf, p0, p1, r0, r1, turn, cyc, spread, perm, drecv, mrecv,
    in_sem, s_rly, s_a, s_b, s_w1, s_w2, s_fw, s_r0, s_r1, s_m, s_d,
    q_rly, q_a, q_w1, q_w2, q_r0, q_r1, q_m, q_d,
):
    rows, cols, depth, chunks = sizes
    r, c, x = lax.axis_index("row"), lax.axis_index("col"), lax.axis_index("rep")
    y, u = c // 2, c % 2
    oy, ou, ox = 1 - y, 1 - u, 1 - x
    sub, kc = a_v.shape[1:]
    width = w_v.shape[1]
    half = kc // 2
    slab = half // chunks
    strip = o_ref.shape[2]
    lanes = o_ref.shape[3]
    groups = width // (cols * strip)
    f32 = jnp.float32

    def rowset(side):
        return pl.ds(pl.multiple_of((x * 2 + side) * sub, sub), sub)

    def khalf(v):
        return pl.ds(v * half, half)

    def side_rows(side):
        return pl.ds(pl.multiple_of(side * half, half), half)

    loads = (
        pltpu.make_async_copy(a_hbm.at[rowset(oy)], a_v.at[0], in_sem.at[0]),
        pltpu.make_async_copy(a_hbm.at[rowset(y)], a_v.at[1], in_sem.at[1]),
        pltpu.make_async_copy(w_hbm.at[side_rows(x)], w_v.at[side_rows(x)], in_sem.at[2]),
        pltpu.make_async_copy(w_hbm.at[side_rows(ox)], w_v.at[side_rows(ox)], in_sem.at[3]),
    )
    for load in loads:
        load.start()

    barrier = pltpu.get_barrier_semaphore()
    total = rows * cols * depth
    me = (r * cols + c) * depth + x

    def greet(step, carry):
        other = (me + step) % total
        pl.semaphore_signal(
            barrier,
            inc=1,
            device_id=(other // (cols * depth), (other // depth) % cols, other % depth),
            device_id_type=MESH,
        )
        return carry

    lax.fori_loop(1, total, greet, 0)

    pl.semaphore_wait(barrier, total - 1)
    loads[0].wait()

    def remote(source, target, send, recv, to):
        return pltpu.make_async_remote_copy(
            src_ref=source, dst_ref=target, send_sem=send, recv_sem=recv,
            device_id=to, device_id_type=MESH,
        )

    def arrived(target, recv):
        pltpu.make_async_copy(target, target, recv).wait()

    pending = []

    def send(source, target, ssem, rsem, to, same=None):
        copy = remote(source, target, ssem, rsem, to)
        if same is None:
            copy.start()
            pending.append((copy, None))
            return

        @pl.when(same)
        def _():
            pltpu.make_async_copy(source, target, rsem).start()

        @pl.when(jnp.logical_not(same))
        def _():
            copy.start()

        pending.append((copy, jnp.logical_not(same)))

    rises = [(v, t) for v in range(2) for t in range(2)]

    def piece(v, t):
        return pl.ds(t * (sub // 2), sub // 2), khalf(v)

    for v, t in rises:
        at, ks = piece(v, t)
        send(
            a_v.at[0, at, ks], relay.at[at, ks], s_rly.at[v, t], q_rly.at[v, t],
            (r, oy * 2 + u, x),
        )
    loads[1].wait()
    for v in range(2):
        send(
            a_v.at[1, :, khalf(v)], abuf.at[r, :, khalf(v)], s_a.at[v], q_a.at[r, v],
            (c, y * 2 + v, x), jnp.logical_and(c == r, u == v),
        )
    loads[2].wait()

    def krows(side, n):
        return pl.ds(pl.multiple_of(side * half + n * slab, slab), slab)

    def wpart(ref, side, n, h):
        return ref.at[krows(side, n), pl.ds(h * lanes, lanes)]

    for h in range(depth):
        for n in range(chunks):
            send(
                wpart(w_v, x, n, h), wpart(wbuf, x, n, h), s_w1.at[h, n], q_w1.at[h, n],
                (r, oy * 2 + u, x),
            )

    far = oy * 2 + u
    for v, t in rises:
        at, ks = piece(v, t)
        arrived(relay.at[at, ks], q_rly.at[v, t])
        send(
            relay.at[at, ks], abuf.at[r, at, ks], s_b.at[v, t], q_a.at[r, v],
            (far, y * 2 + v, x), jnp.logical_and(far == r, u == v),
        )
    loads[3].wait()

    src = lax.broadcasted_iota(jnp.int32, (2 * width, 2 * width), 0)
    dst = lax.broadcasted_iota(jnp.int32, (2 * width, 2 * width), 1)
    lane_in = dst % strip
    grp = (dst // strip) % groups
    blk = (dst // (strip * groups)) % 2
    own = dst // (2 * strip * groups)
    perm[...] = jnp.where(
        src == blk * width + grp * (cols * strip) + own * strip + lane_in, 1.0, 0.0
    ).astype(jnp.bfloat16)

    order = (r, r + 1 - 2 * (r % 2), (r + rows // 2) % rows, rows - 1 - r)

    def forward_w(h, n):
        arrived(wpart(wbuf, x, n, h), q_w1.at[h, n])
        send(
            wpart(wbuf, x, n, h), wpart(wbuf, x, n, h), s_w2.at[h, n], q_w2.at[h, n], (r, c, ox)
        )

    def forward_a(i):
        mine = side_rows(u)
        arrived(abuf.at[i, :, mine], q_a.at[i, u])
        send(abuf.at[i, :, mine], abuf.at[i, :, mine], s_fw.at[i], q_a.at[i, u], (r, y * 2 + ou, x))

    def product(d):
        i = order[d]
        arrived(abuf.at[i, :, side_rows(ou)], q_a.at[i, ou])
        p0[i] = jnp.dot(abuf[i], w_v[...], preferred_element_type=f32)
        if d > 0:
            send(p0.at[i], r0.at[r], s_r0.at[i], q_r0.at[r], (i, c, x))

    hops = [(h, n) for h in range(depth) for n in range(chunks)]
    each = len(hops) // rows
    for d in range(rows):
        forward_a(order[d])
        product(d)
        for h, n in hops[d * each:(d + 1) * each]:
            forward_w(h, n)

    def add_product(side, n, h, first):
        part = jnp.dot(
            abuf[:, :, krows(side, n)].reshape(rows * sub, slab),
            wbuf[krows(side, n), pl.ds(h * lanes, lanes)],
            preferred_element_type=f32,
        ).reshape(rows, sub, lanes)
        p1[h] = part if first else p1[h] + part

    def other_product(h):
        for n in range(chunks):
            add_product(x, n, h, n == 0)
        for n in range(chunks):
            arrived(wpart(wbuf, ox, n, h), q_w2.at[h, n])
            add_product(ox, n, h, False)
        for d in range(1, rows):
            i = order[d]
            send(p1.at[h, i], r1.at[h, r], s_r1.at[h, i], q_r1.at[h, r], (i, c, x))

    def mirror(q, block, px):
        owner = block * 2 + u
        for pu in range(2):
            same = jnp.logical_and(jnp.logical_and(owner == r, px == x), pu == u)
            send(
                cyc.at[block, pl.ds(pu * strip, strip), pl.ds(px * lanes, lanes)],
                mrecv.at[r * depth + x],
                s_m.at[q, px, pu], q_m.at[r * depth + x], (owner, y * 2 + pu, px), same,
            )

    def finish_own():
        value = p0[r]
        for d in range(1, rows):
            i = order[d]
            arrived(r0.at[i], q_r0.at[i])
            value = value + r0[i]
        value = value.astype(jnp.bfloat16)
        cyc[y] = value
        for px in range(depth):
            mirror(0, y, px)
        rows_of = pl.ds(pl.multiple_of(y * width, width), width)
        turn[...] = jnp.dot(value, perm[rows_of, :], preferred_element_type=f32)

    def finish_other(h):
        value = p1[h, r]
        for d in range(1, rows):
            i = order[d]
            arrived(r1.at[h, i], q_r1.at[h, i])
            value = value + r1[h, i]
        value = value.astype(jnp.bfloat16)
        cyc[oy, :, pl.ds(h * lanes, lanes)] = value
        mirror(1, oy, h)
        rows_of = pl.ds(pl.multiple_of(oy * width + h * lanes, lanes), lanes)
        return turn[...] + jnp.dot(value, perm[rows_of, :], preferred_element_type=f32)

    other_product(0)
    finish_own()
    for h in range(1, depth):
        other_product(h)
        turn[...] = finish_other(h - 1)
    turned = finish_other(depth - 1)

    for to in range(cols):
        spread[to] = turned[:, to * lanes:(to + 1) * lanes].astype(jnp.bfloat16)
    place = pl.ds(pl.multiple_of(y * sub, sub), sub)
    for to in range(cols):
        send(spread.at[to], drecv.at[u, place, :], s_d.at[to], q_d.at[u, y], (r, to, x), c == to)

    for i in range(rows * depth):
        arrived(mrecv.at[i], q_m.at[i])
    for pu in range(2):
        for py in range(2):
            arrived(drecv.at[pu, pl.ds(py * sub, sub), :], q_d.at[pu, py])
        flipped = jnp.transpose(drecv[pu].astype(f32))
        for py in range(2):
            for g in range(groups):
                at = (py * groups + g) * strip
                a = (py * 2 + pu) * groups + g
                o_ref[a, 0] = mrecv[a].astype(f32) + flipped[at:at + strip, :]

    for copy, sent in pending:
        if sent is None:
            copy.wait_send()
        else:
            pl.when(sent)(copy.wait_send)


def planned(sizes, amplitudes, intermediate):
    rows, cols, depth, chunks = sizes
    band, kc = amplitudes.shape
    width = intermediate.shape[1]
    sub = band // (2 * depth)
    owners = rows * depth
    strip = width // owners
    lanes = band // depth
    bf16, f32 = jnp.bfloat16, jnp.float32
    dma = pltpu.SemaphoreType.DMA
    return pl.pallas_call(
        functools.partial(kernel, sizes),
        out_shape=jax.ShapeDtypeStruct((owners, 1, strip, lanes), f32),
        in_specs=[pl.BlockSpec(memory_space=pl.ANY)] * 2,
        out_specs=pl.BlockSpec(memory_space=pltpu.VMEM),
        scratch_shapes=[
            pltpu.VMEM((2, sub, kc), bf16),
            pltpu.VMEM((kc, width), bf16),
            pltpu.VMEM((sub, kc), bf16),
            pltpu.VMEM((rows, sub, kc), bf16),
            pltpu.VMEM((kc, width), bf16),
            pltpu.VMEM((rows, sub, width), f32),
            pltpu.VMEM((depth, rows, sub, lanes), f32),
            pltpu.VMEM((rows, sub, width), f32),
            pltpu.VMEM((depth, rows, sub, lanes), f32),
            pltpu.VMEM((sub, 2 * width), f32),
            pltpu.VMEM((2, sub, width), bf16),
            pltpu.VMEM((cols, sub, lanes), bf16),
            pltpu.VMEM((2 * width, 2 * width), bf16),
            pltpu.VMEM((2, 2 * sub, lanes), bf16),
            pltpu.VMEM((owners, strip, lanes), bf16),
            dma((4,)), dma((2, 2)), dma((2,)), dma((2, 2)), dma((depth, chunks)), dma((depth, chunks)),
            dma((rows,)), dma((rows,)), dma((depth, rows)), dma((2, depth, 2)), dma((cols,)),
            dma((2, 2)), dma((rows, 2)), dma((depth, chunks)), dma((depth, chunks)),
            dma((rows,)), dma((depth, rows)), dma((owners,)), dma((2, 2)),
        ],
        compiler_params=pltpu.CompilerParams(collective_id=0, has_side_effects=True),
    )(amplitudes, intermediate)


def solution(mesh):
    rows, cols, depth = (mesh.shape[name] for name in ("row", "col", "rep"))

    def local(amplitudes, intermediate):
        square = rows == cols == 2 * depth and depth == 2
        fits = amplitudes.shape[0] == intermediate.shape[1]
        if square and fits:
            return planned((rows, cols, depth, 4), amplitudes, intermediate)
        return general(amplitudes, intermediate)

    in_specs = (P("row", "col"), P("row", "col"))
    out_specs = P(None, "col", None, ("row", "rep"))
    return jax.shard_map(local, mesh=mesh, in_specs=in_specs, out_specs=out_specs, check_vma=False)
```

time: 45.1 us -> 42.5 us (0.942)
  the two profiles are of different devices: /device:TPU:5 before, /device:TPU:0 now
where the time goes in v2:
time: 42.5 us; the launch traced here: 42.3 us
  Pallas kernels  40.8 us (96%)
  local copies, waits for them, and re-layouts  1.57 us (4%)
    pallas_call x1, Pallas kernels, planned(): pl.pallas_call(functools.partial(kernel, sizes), out_shape=jax.ShapeDtype...  40.8 us
    unnamed x1, local copies, waits for them, and re-layouts  1.57 us

profile of v2, /device:TPU:0, one launch (start us, length us, event | category | flops | bytes accessed | tf_op | source)
XLA Modules:
  0.0 42.3 jit_solution(7766114644487843671)
XLA Ops:
  0.0 40.8 %shard_map.28 = f32[8,1,32,128]{3,2,1,0:T(8,128)} custom-call(bf16[256,2048]{1,0:T(8,128)(2,1)} %a_hbm.1, bf16[2048,256]{1,0:T(8,128)(2,1)} %w_hbm.1), custom_call_target="tpu_custom_call" | custom-call | tf_op jit(solution)/shard_map/pallas_call | solution.py:308
  40.8 1.6 %copy.4 = f32[8,1,32,128]{3,2,1,0:T(8,128)} copy(f32[8,1,32,128]{3,2,1,0:T(8,128)} %shard_map.28) | data formatting | bytes 262144

commit v3 on v2

--- a/solution.py
+++ b/solution.py
@@ -130,10 +130,10 @@
 
         pending.append((copy, jnp.logical_not(same)))
 
-    rises = [(v, t) for v in range(2) for t in range(2)]
+    rises = [(v, t) for v in range(2) for t in range(4)]
 
     def piece(v, t):
-        return pl.ds(t * (sub // 2), sub // 2), khalf(v)
+        return pl.ds(t * (sub // 4), sub // 4), khalf(v)
 
     for v, t in rises:
         at, ks = piece(v, t)
@@ -326,9 +326,9 @@
             pltpu.VMEM((2 * width, 2 * width), bf16),
             pltpu.VMEM((2, 2 * sub, lanes), bf16),
             pltpu.VMEM((owners, strip, lanes), bf16),
-            dma((4,)), dma((2, 2)), dma((2,)), dma((2, 2)), dma((depth, chunks)), dma((depth, chunks)),
+            dma((4,)), dma((2, 4)), dma((2,)), dma((2, 4)), dma((depth, chunks)), dma((depth, chunks)),
             dma((rows,)), dma((rows,)), dma((depth, rows)), dma((2, depth, 2)), dma((cols,)),
-            dma((2, 2)), dma((rows, 2)), dma((depth, chunks)), dma((depth, chunks)),
+            dma((2, 4)), dma((rows, 2)), dma((depth, chunks)), dma((depth, chunks)),
             dma((rows,)), dma((depth, rows)), dma((owners,)), dma((2, 2)),
         ],
         compiler_params=pltpu.CompilerParams(collective_id=0, has_side_effects=True),

time: 42.5 us -> 42.2 us (level)
  no operation moved by 1% of the time
where the time goes in v3:
time: 42.2 us; the launch traced here: 42.1 us
  Pallas kernels  40.5 us (96%)
  local copies, waits for them, and re-layouts  1.57 us (4%)
    pallas_call x1, Pallas kernels, planned(): pl.pallas_call(functools.partial(kernel, sizes), out_shape=jax.ShapeDtype...  40.5 us
    unnamed x1, local copies, waits for them, and re-layouts  1.57 us

profile of v3, /device:TPU:0, one launch (start us, length us, event | category | flops | bytes accessed | tf_op | source)
XLA Modules:
  0.0 42.1 jit_solution(4270340389657369035)
XLA Ops:
  0.0 40.5 %shard_map.28 = f32[8,1,32,128]{3,2,1,0:T(8,128)} custom-call(bf16[256,2048]{1,0:T(8,128)(2,1)} %a_hbm.1, bf16[2048,256]{1,0:T(8,128)(2,1)} %w_hbm.1), custom_call_target="tpu_custom_call" | custom-call | tf_op jit(solution)/shard_map/pallas_call | solution.py:308
  40.5 1.6 %copy.4 = f32[8,1,32,128]{3,2,1,0:T(8,128)} copy(f32[8,1,32,128]{3,2,1,0:T(8,128)} %shard_map.28) | data formatting | bytes 262144
